TPU v7x, 32 devices: a whole 2x2x4 slice. The times are simulated.
32 devices in a mesh: dp: 4 (over y, x), frame: 2 (over core), tensor: 4 (over z).
Axes of the slice: x: 2, y: 2, z: 4, core: 2. Of those that a mesh axis runs over, the one named last changes fastest.
Arguments:
- tokens: bfloat16 [8, 8, 256, 1024], P('dp', ('frame', 'tensor')), may hold values from -6 to 6
- out_grad: bfloat16 [8, 8, 256, 1024], P('dp', ('frame', 'tensor')), may hold values from -6 to 6
- noise_index: int32 [8, 8], P('dp', 'frame'), may hold values from 0 to 999, as said below
- qkv_weight: bfloat16 [1024, 3, 1024], P(('dp', 'frame'), None, 'tensor'), may hold values from -0.1875 to 0.1875
- out_weight: bfloat16 [1024, 1024], P(('dp', 'frame'), 'tensor'), may hold values from -0.75 to 0.75
- up_weight: bfloat16 [1024, 4096], P(('dp', 'frame'), 'tensor'), may hold values from -0.1875 to 0.1875
- down_weight: bfloat16 [1024, 4096], P(('dp', 'frame'), 'tensor'), may hold values from -0.09375 to 0.09375
- ada_weight: bfloat16 [1024, 6, 1024], P(('dp', 'frame'), None, 'tensor'), may hold values from -0.25 to 0.25
Outputs:
- result: bfloat16 [8, 8, 256, 1024], P('dp', ('frame', 'tensor'))
- input_grad: bfloat16 [8, 8, 256, 1024], P('dp', ('frame', 'tensor'))
- qkv_grad: float32 [1024, 3, 1024], P(('dp', 'frame'), None, 'tensor')
- out_weight_grad: float32 [1024, 1024], P(('dp', 'frame'), 'tensor')
- up_grad: float32 [1024, 4096], P(('dp', 'frame'), 'tensor')
- down_grad: float32 [1024, 4096], P(('dp', 'frame'), 'tensor')
- ada_grad: float32 [1024, 6, 1024], P(('dp', 'frame'), None, 'tensor')
Inputs may be any that keep to these rules, and one draw needn't show every extreme that they name: `noise_index`: each frame's noise level, most often near 1000 - 1.
All inputs are finite; a program needn't handle non-finite values.
Results may differ from a plain program's by a relative error of at most 0.018.
Values may be sent and summed in bfloat16 or wider, within the bound.
A program may use at most 192 MiB of HBM per device.

v0:
```python
import math
import jax
import jax.numpy as jnp
from jax import lax
from jax.sharding import PartitionSpec as P

HEAD_DIM = 64
epsilon = 1e-06
highest = lax.Precision.HIGHEST


def normalize(values):
    center = values - jnp.mean(values, axis=-1, keepdims=True)
    spread = jnp.mean(center * center, axis=-1, keepdims=True)
    inverse = lax.rsqrt(spread + epsilon)
    return (center * inverse, inverse)


def norm_back(upstream, normed, inverse):
    upstream_mean = jnp.mean(upstream, axis=-1, keepdims=True)
    product_mean = jnp.mean(upstream * normed, axis=-1, keepdims=True)
    return inverse * (upstream - upstream_mean - normed * product_mean)


def level_embedding(levels, model_width):
    halfway = model_width // 2
    frequency = jnp.exp(-math.log(10000.0) * jnp.arange(halfway, dtype=jnp.float32) / halfway)
    angles = levels.astype(jnp.float32)[..., None] * frequency
    return jnp.concatenate([jnp.cos(angles), jnp.sin(angles)], axis=-1)


def gelu_tanh(values):
    return jax.nn.gelu(values, approximate=True)


def on_device(
    tokens, out_grad, noise_index, qkv_weight, out_weight, up_weight, down_weight, ada_weight
):
    clips = tokens.shape[0]
    patches = tokens.shape[2]
    model_width = tokens.shape[-1]
    local_width = qkv_weight.shape[2]
    rows_here = qkv_weight.shape[0]
    heads_here = local_width // HEAD_DIM
    scaling = HEAD_DIM ** (-0.5)
    groups = lax.axis_size("tensor")
    halves = lax.axis_size("frame")
    replicas = lax.axis_size("dp")
    with jax.named_scope("modulation"):
        levels_all = lax.all_gather(noise_index, ("dp", "frame"), axis=0, tiled=True)
        levels_all = levels_all.reshape(replicas * halves, clips, groups)
        condition_all = jax.nn.silu(level_embedding(levels_all, model_width)).astype(jnp.bfloat16)
        row_block = lax.axis_index("dp") * halves + lax.axis_index("frame")
        my_condition = lax.dynamic_slice_in_dim(
            condition_all, row_block * rows_here, rows_here, axis=3
        )
        partial_mod = jnp.einsum(
            "acgd,dkw->acgkw", my_condition, ada_weight, preferred_element_type=jnp.float32
        )
        summed_mod = lax.psum_scatter(
            partial_mod, ("dp", "frame"), scatter_dimension=0, tiled=True
        )[0]
        modulation = lax.all_to_all(summed_mod, "tensor", 1, 3, tiled=True)
        modulation = modulation.reshape(clips, 6, 1, model_width)
    with jax.named_scope("weights"):
        joint_weight, mixer_weight, upward_weight, downward_weight = (
            lax.all_gather(w, ("dp", "frame"), axis=0, tiled=True)
            for w in (qkv_weight, out_weight, up_weight, down_weight)
        )
    residual = tokens[:, 0].astype(jnp.float32)
    upstream = out_grad[:, 0].astype(jnp.float32)
    shift1, scale1, gate1 = (modulation[:, 0], modulation[:, 1], modulation[:, 2])
    shift2, scale2, gate2 = (modulation[:, 3], modulation[:, 4], modulation[:, 5])

    def gather_tokens(values):
        return lax.all_gather(values, "tensor", axis=1, tiled=True)

    def scatter_tokens(values):
        return lax.psum_scatter(
            values.astype(jnp.bfloat16), "tensor", scatter_dimension=1, tiled=True
        ).astype(jnp.float32)

    with jax.named_scope("forward"):
        normed_one, inverse_one = normalize(residual)
        entering_one = (normed_one * (1.0 + scale1) + shift1).astype(jnp.bfloat16)
        flat_one = gather_tokens(entering_one)
        token_count = flat_one.shape[1]
        projected = jnp.einsum(
            "crd,dkh->crkh", flat_one, joint_weight, preferred_element_type=jnp.float32
        ).astype(jnp.bfloat16)
        queries = projected[:, :, 0]
        keys_all = lax.all_gather(projected[:, :, 1], "frame", axis=1, tiled=True)
        values_all = lax.all_gather(projected[:, :, 2], "frame", axis=1, tiled=True)
        key_heads = keys_all.reshape(clips, -1, heads_here, HEAD_DIM)
        value_heads = values_all.reshape(clips, -1, heads_here, HEAD_DIM)
        block_rows = min(512, token_count)
        block_count = token_count // block_rows
        query_blocks = jnp.moveaxis(
            queries.reshape(clips, block_count, block_rows, heads_here, HEAD_DIM), 1, 0
        )

        def attend(query_block):
            scores = (
                jnp.einsum(
                    "cqhe,ckhe->chqk", query_block, key_heads, preferred_element_type=jnp.float32
                )
                * scaling
            )
            largest = jnp.max(scores, axis=-1, keepdims=True)
            raised = jnp.exp(scores - largest)
            totals_row = jnp.sum(raised, axis=-1, keepdims=True)
            probs_low = (raised / totals_row).astype(jnp.bfloat16)
            outputs = jnp.einsum(
                "chqk,ckhe->cqhe", probs_low, value_heads, preferred_element_type=jnp.float32
            )
            return (outputs.astype(jnp.bfloat16), (largest + jnp.log(totals_row))[..., 0])

        attended_blocks, log_totals = lax.map(attend, query_blocks)
        attended = jnp.moveaxis(attended_blocks, 0, 1).reshape(clips, token_count, local_width)
        partial_one = jnp.einsum(
            "crh,oh->cro", attended, mixer_weight, preferred_element_type=jnp.float32
        )
        branch_one = scatter_tokens(partial_one)
        middle = residual + gate1 * branch_one
        normed_two, inverse_two = normalize(middle)
        entering_two = (normed_two * (1.0 + scale2) + shift2).astype(jnp.bfloat16)
        flat_two = gather_tokens(entering_two)
        up_values = jnp.einsum(
            "crd,df->crf", flat_two, upward_weight, preferred_element_type=jnp.float32
        )
        hidden = gelu_tanh(up_values).astype(jnp.bfloat16)
        partial_two = jnp.einsum(
            "crf,of->cro", hidden, downward_weight, preferred_element_type=jnp.float32
        )
        branch_two = scatter_tokens(partial_two)
        output = (middle + gate2 * branch_two).astype(jnp.bfloat16)
    with jax.named_scope("backward_ffn"):
        grad_gate_two = jnp.sum(upstream * branch_two, axis=1)
        grad_branch_two = (gate2 * upstream).astype(jnp.bfloat16)
        grad_two_all = gather_tokens(grad_branch_two)
        grad_hidden = jnp.einsum(
            "cro,of->crf", grad_two_all, downward_weight, preferred_element_type=jnp.float32
        )
        down_total = jnp.einsum(
            "cro,crf->of", grad_two_all, hidden, preferred_element_type=jnp.float32
        )
        _, gelu_pullback = jax.vjp(gelu_tanh, up_values)
        grad_up = gelu_pullback(grad_hidden)[0].astype(jnp.bfloat16)
        up_total = jnp.einsum("crd,crf->df", flat_two, grad_up, preferred_element_type=jnp.float32)
        partial_back_two = jnp.einsum(
            "crf,df->crd", grad_up, upward_weight, preferred_element_type=jnp.float32
        )
        grad_entering_two = scatter_tokens(partial_back_two)
        grad_shift_two = jnp.sum(grad_entering_two, axis=1)
        grad_scale_two = jnp.sum(grad_entering_two * normed_two, axis=1)
        grad_middle = upstream + norm_back(
            grad_entering_two * (1.0 + scale2), normed_two, inverse_two
        )
        grad_gate_one = jnp.sum(grad_middle * branch_one, axis=1)
    with jax.named_scope("backward_attention"):
        grad_branch_one = (gate1 * grad_middle).astype(jnp.bfloat16)
        grad_one_all = gather_tokens(grad_branch_one)
        grad_attended = jnp.einsum(
            "cro,oh->crh", grad_one_all, mixer_weight, preferred_element_type=jnp.float32
        ).astype(jnp.bfloat16)
        mixer_total = jnp.einsum(
            "cro,crh->oh", grad_one_all, attended, preferred_element_type=jnp.float32
        )
        grad_blocks = jnp.moveaxis(
            grad_attended.reshape(clips, block_count, block_rows, heads_here, HEAD_DIM), 1, 0
        )

        def attend_back(carried, pieces):
            key_sum, value_sum = carried
            query_block, grad_block, log_block = pieces
            scores = (
                jnp.einsum(
                    "cqhe,ckhe->chqk", query_block, key_heads, preferred_element_type=jnp.float32
                )
                * scaling
            )
            probs = jnp.exp(scores - log_block[..., None])
            grad_probs = jnp.einsum(
                "cqhe,ckhe->chqk", grad_block, value_heads, preferred_element_type=jnp.float32
            )
            value_sum = value_sum + jnp.einsum(
                "chqk,cqhe->ckhe",
                probs.astype(jnp.bfloat16),
                grad_block,
                preferred_element_type=jnp.float32,
            )
            row_terms = jnp.sum(probs * grad_probs, axis=-1, keepdims=True)
            grad_scores = (probs * (grad_probs - row_terms)).astype(jnp.bfloat16)
            grad_queries = (
                jnp.einsum(
                    "chqk,ckhe->cqhe", grad_scores, key_heads, preferred_element_type=jnp.float32
                )
                * scaling
            )
            key_sum = (
                key_sum
                + jnp.einsum(
                    "chqk,cqhe->ckhe", grad_scores, query_block, preferred_element_type=jnp.float32
                )
                * scaling
            )
            return ((key_sum, value_sum), grad_queries)

        zeros_keys = jnp.zeros(key_heads.shape, jnp.float32)
        (key_grads, value_grads), query_grads = lax.scan(
            attend_back, (zeros_keys, zeros_keys), (query_blocks, grad_blocks, log_totals)
        )
        query_grads = jnp.moveaxis(query_grads, 0, 1).reshape(clips, token_count, local_width)
        key_own, value_own = (
            lax.psum_scatter(
                grads.reshape(clips, -1, local_width).astype(jnp.bfloat16),
                "frame",
                scatter_dimension=1,
                tiled=True,
            ).astype(jnp.float32)
            for grads in (key_grads, value_grads)
        )
        grad_projected = jnp.stack([query_grads, key_own, value_own], axis=2).astype(jnp.bfloat16)
        joint_total = jnp.einsum(
            "crd,crkh->dkh", flat_one, grad_projected, preferred_element_type=jnp.float32
        )
        partial_back_one = jnp.einsum(
            "crkh,dkh->crd", grad_projected, joint_weight, preferred_element_type=jnp.float32
        )
        grad_entering_one = scatter_tokens(partial_back_one)
        grad_shift_one = jnp.sum(grad_entering_one, axis=1)
        grad_scale_one = jnp.sum(grad_entering_one * normed_one, axis=1)
        grad_input = grad_middle + norm_back(
            grad_entering_one * (1.0 + scale1), normed_one, inverse_one
        )
    with jax.named_scope("ada_grad"):
        grad_modulation = jnp.stack(
            [
                grad_shift_one,
                grad_scale_one,
                grad_gate_one,
                grad_shift_two,
                grad_scale_two,
                grad_gate_two,
            ],
            axis=1,
        )
        grad_columns = lax.all_to_all(
            grad_modulation.reshape(clips, 1, 6, model_width), "tensor", 3, 1, tiled=True
        )
        grad_all = lax.all_gather(grad_columns, ("dp", "frame"), axis=0, tiled=True)
        grad_all = grad_all.reshape(replicas * halves, clips, groups, 6, local_width)
        adaptive_total = jnp.einsum(
            "acgd,acgkw->dkw", my_condition.astype(jnp.float32), grad_all, precision=highest
        )
    with jax.named_scope("weight_grads"):
        summed = tuple(
            (
                lax.psum_scatter(
                    total.astype(jnp.bfloat16), ("dp", "frame"), scatter_dimension=0, tiled=True
                ).astype(jnp.float32)
                for total in (joint_total, mixer_total, up_total, down_total)
            )
        )
    result = output[:, None]
    input_grad = grad_input.astype(jnp.bfloat16)[:, None]
    return (result, input_grad, summed[0], summed[1], summed[2], summed[3], adaptive_total)


def solution(mesh):
    return jax.shard_map(
        on_device,
        mesh=mesh,
        in_specs=(
            P("dp", ("frame", "tensor"), None, None),
            P("dp", ("frame", "tensor"), None, None),
            P("dp", "frame"),
            P(("dp", "frame"), None, "tensor"),
            P(("dp", "frame"), "tensor"),
            P(("dp", "frame"), "tensor"),
            P(("dp", "frame"), "tensor"),
            P(("dp", "frame"), None, "tensor"),
        ),
        out_specs=(
            P("dp", ("frame", "tensor"), None, None),
            P("dp", ("frame", "tensor"), None, None),
            P(("dp", "frame"), None, "tensor"),
            P(("dp", "frame"), "tensor"),
            P(("dp", "frame"), "tensor"),
            P(("dp", "frame"), "tensor"),
            P(("dp", "frame"), None, "tensor"),
        ),
        check_vma=False,
    )
```

profile of v0, /device:TPU:0, one launch (start us, length us, event | category | flops | bytes accessed | tf_op | source)
XLA Modules:
  0.0 1416.2 jit_solution(16636748688124716342)
XLA Ops:
  7.3 10.7 all-gather.3
  24.1 50.8 %all-reduce.3.cloned.1.call-done = f32[8,2,4,6,256]{4,2,3,1,0:T(4,128)} async-done(((f32[8,2,4,6,256]{4,2,3,1,0:T(4,128)}), f32[8,2,4,6,256]{4,2,3,1,0:T(4,128)}) %all-reduce.3.cloned.1.call-update) | async-done | bytes 393232
  89.4 12.3 all-gather.16.cloned.1.call-done
  101.8 82.9 %all-gather.14.cloned.1.call-done = bf16[2,1024,1024]{2,1,0:T(8,128)(2,1)} async-done(((bf16[2,256,1024]{2,1,0:T(8,128)(2,1)}), bf16[2,1024,1024]{2,1,0:T(8,128)(2,1)}) %all-gather.14.cloned.1.call-update) | async-done | bytes 4194320 | tf_op jit(solution)/shard_map/forward/all_gather | solution.py:76
  184.7 6.1 fusion.57
  193.1 11.0 all_gather.41
  217.8 87.8 %while.27 = (s32[]{:T(128)}, bf16[2,2,512,4,64]{2,4,3,1,0:T(8,128)(2,1)}, f32[2,2,4,512]{3,2,1,0:T(4,128)S(1)}, bf16[2,2,512,4,64]{2,4,3,1,0:T(8,128)(2,1)}, bf1...) while((s32[]{:T(128)}, bf16[2,2,512,4,64]{2,4,3,1,0:T(8,128)(2,1)}, ...), condition=%wide.region_6.7_spmd, body=%wide.region_3.6_spmd.sunk | while | flops 2223239168 | bytes 106037344 | solution.py:118
  217.8 14.3 %multiply_reduce_fusion.5 = (f32[2,4,512]{2,1,0:T(4,128)S(1)}, f32[2,4,512,2048]{3,2,1,0:T(8,128)}) fusion(bf16[2,2048,4,64]{1,3,2,0:T(8,128)(2,1)S(1)} %get-tuple-element.435, bf16[2,2,512,4,64]{2,4,3,1,0:T(8,128)(2,1)} %get-tuple-element.434, s32[]{:T(128)S(6)} %copy.212), kind=kOutput, calls=%fused_computation.2.clone.1 | convolution fusion | flops 1090514944 | bytes 36192260 | tf_op jit(solution)/shard_map/forward/while/body/eval_jaxpr/cqhe,ckhe->chqk/dot_general | solution.py:104
  232.1 14.0 fusion.138
  246.1 15.5 %fusion.139 = bf16[2,2,512,4,64]{2,4,3,1,0:T(8,128)(2,1)} fusion(bf16[2,2,512,4,64]{2,4,3,1,0:T(8,128)(2,1)} %get-tuple-element.425, s32[]{:T(128)S(6)} %copy.212, bf16[2,2048,4,64]{1,3,2,0:T(8,128)(2,1)} %get-tuple-element.436, f32[2,4,512,2048]{3,2,1,0:T(8,128)} %get-tuple-element.404, f32[2,4,512]{2,1,0:T(4,128)S(1)} %fusion.138, ...), kind=kOutput, calls=%fused_computation.7.clone.1 | convolution fusion | flops 1107558400 | bytes 36208644 | tf_op jit(solution)/shard_map/forward/while/body/eval_jaxpr/chqk,ckhe->cqhe/dot_general | solution.py:113
  261.7 14.3 %multiply_reduce_fusion.5 = (f32[2,4,512]{2,1,0:T(4,128)S(1)}, f32[2,4,512,2048]{3,2,1,0:T(8,128)}) fusion(bf16[2,2048,4,64]{1,3,2,0:T(8,128)(2,1)S(1)} %get-tuple-element.435, bf16[2,2,512,4,64]{2,4,3,1,0:T(8,128)(2,1)} %get-tuple-element.434, s32[]{:T(128)S(6)} %copy.212), kind=kOutput, calls=%fused_computation.2.clone.1 | convolution fusion | flops 1090514944 | bytes 36192260 | tf_op jit(solution)/shard_map/forward/while/body/eval_jaxpr/cqhe,ckhe->chqk/dot_general | solution.py:104
  276.0 14.0 fusion.138
  290.0 15.5 %fusion.139 = bf16[2,2,512,4,64]{2,4,3,1,0:T(8,128)(2,1)} fusion(bf16[2,2,512,4,64]{2,4,3,1,0:T(8,128)(2,1)} %get-tuple-element.425, s32[]{:T(128)S(6)} %copy.212, bf16[2,2048,4,64]{1,3,2,0:T(8,128)(2,1)} %get-tuple-element.436, f32[2,4,512,2048]{3,2,1,0:T(8,128)} %get-tuple-element.404, f32[2,4,512]{2,1,0:T(4,128)S(1)} %fusion.138, ...), kind=kOutput, calls=%fused_computation.7.clone.1 | convolution fusion | flops 1107558400 | bytes 36208644 | tf_op jit(solution)/shard_map/forward/while/body/eval_jaxpr/chqk,ckhe->cqhe/dot_general | solution.py:113
  317.2 76.9 %reduce-scatter.11.cloned.1.call-done = bf16[2,256,1024]{2,1,0:T(8,128)(2,1)} async-done(((bf16[2,1024,1024]{2,1,0:T(8,128)(2,1)}), bf16[2,256,1024]{2,1,0:T(8,128)(2,1)}) %reduce-scatter.11.cloned.1.call-update) | async-done | bytes 1048592 | tf_op jit(solution)/shard_map/forward/reduce_scatter | solution.py:79
  404.6 19.7 %all-gather.20.cloned.1.call-done = bf16[1024,1024]{1,0:T(8,128)(2,1)} async-done(((bf16[128,1024]{1,0:T(8,128)(2,1)}), bf16[1024,1024]{1,0:T(8,128)(2,1)}) %all-gather.20.cloned.1.call-update) | async-done | bytes 2097168 | tf_op jit(solution)/shard_map/weights/all_gather | solution.py:67
  424.3 82.9 %all-gather.18.cloned.1.call-done = bf16[2,1024,1024]{2,1,0:T(8,128)(2,1)} async-done(((bf16[2,256,1024]{2,1,0:T(8,128)(2,1)}), bf16[2,1024,1024]{2,1,0:T(8,128)(2,1)}) %all-gather.18.cloned.1.call-update) | async-done | bytes 4194320 | tf_op jit(solution)/shard_map/forward/all_gather | solution.py:76
  507.2 10.6 fusion.81
  517.9 17.6 %all-gather.22.cloned.1.call-done = bf16[1024,1024]{1,0:T(8,128)(2,1)} async-done(((bf16[128,1024]{1,0:T(8,128)(2,1)}), bf16[1024,1024]{1,0:T(8,128)(2,1)}) %all-gather.22.cloned.1.call-update) | async-done | bytes 2097168 | tf_op jit(solution)/shard_map/weights/all_gather | solution.py:67
  535.4 82.2 %all-gather.24.cloned.1.call-done = bf16[2,1024,1024]{2,1,0:T(8,128)(2,1)} async-done(((bf16[2,256,1024]{2,1,0:T(8,128)(2,1)}), bf16[2,1024,1024]{2,1,0:T(8,128)(2,1)}) %all-gather.24.cloned.1.call-update) | async-done | bytes 4194320 | tf_op jit(solution)/shard_map/backward_ffn/all_gather | solution.py:76
  617.6 12.5 fusion.40
  632.1 6.3 convolution_convert_fusion
  638.7 75.2 %reduce-scatter.15.cloned.1.call-done = bf16[2,256,1024]{2,1,0:T(8,128)(2,1)} async-done(((bf16[2,1024,1024]{2,1,0:T(8,128)(2,1)}), bf16[2,256,1024]{2,1,0:T(8,128)(2,1)}) %reduce-scatter.15.cloned.1.call-update) | async-done | bytes 1048592 | tf_op jit(solution)/shard_map/backward_ffn/reduce_scatter | solution.py:79
  721.0 81.3 %all-gather.26.cloned.1.call-done = bf16[2,1024,1024]{2,1,0:T(8,128)(2,1)} async-done(((bf16[2,256,1024]{2,1,0:T(8,128)(2,1)}), bf16[2,1024,1024]{2,1,0:T(8,128)(2,1)}) %all-gather.26.cloned.1.call-update) | async-done | bytes 4194320 | tf_op jit(solution)/shard_map/backward_attention/all_gather | solution.py:76
  814.1 200.8 %while.28 = (s32[]{:T(128)}, f32[2,2048,4,64]{1,3,2,0:T(8,128)}, f32[2,2048,4,64]{1,3,2,0:T(8,128)}, bf16[2,2,512,4,64]{2,4,3,1,0:T(8,128)(2,1)}, bf16[2,2,512,4...) while((s32[]{:T(128)}, f32[2,2048,4,64]{1,3,2,0:T(8,128)}, ...), condition=%wide.region_16.17_spmd.clone, body=%wide.region_14.16_spmd.clone.sunk | while | flops 5474873344 | bytes 345096384 | solution.py:210
  814.1 14.3 %fusion.149 = f32[2,4,512,2048]{3,2,1,0:T(8,128)} fusion(bf16[2,2048,4,64]{1,3,2,0:T(8,128)(2,1)S(1)} %get-tuple-element.465, bf16[2,2,512,4,64]{2,4,3,1,0:T(8,128)(2,1)} %get-tuple-element.464, s32[]{:T(128)S(6)} %copy.222), kind=kOutput, calls=%fused_computation.30.clone.1 | convolution fusion | flops 1073741824 | bytes 36175876 | tf_op jit(solution)/shard_map/backward_attention/while/body/eval_jaxpr/cqhe,ckhe->chqk/dot_general | solution.py:177
  828.4 16.1 %bitcast_add_fusion.5 = f32[2,2048,4,64]{1,3,2,0:T(8,128)} fusion(f32[2,2048,4,64]{1,3,2,0:T(8,128)} %get-tuple-element.451, f32[2,4,512,2048]{3,2,1,0:T(8,128)} %fusion.149, f32[2,4,512]{2,1,0:T(4,128)S(1)} %dynamic-slice_bitcast_fusion.3, pred[]{:T(512)S(6)} %compare.3, bf16[2,2,512,4,64]{2,4,3,1,0:T(8,128)(2,1)} %get-tuple-element.467, s32[]{:T(128)S(6)} %copy.222), kind=kOutput, calls=%fused_computation.21.clone.1 | convolution fusion | flops 1101004800 | bytes 42483716 | tf_op jit(solution)/shard_map/backward_attention/while/body/eval_jaxpr/chqk,cqhe->ckhe/dot_general | solution.py:186
  844.4 23.8 %multiply_reduce_fusion.6 = (f32[2,4,512]{2,1,0:T(4,128)S(1)}, f32[2,4,512,2048]{3,2,1,0:T(8,128)}) fusion(f32[2,4,512,2048]{3,2,1,0:T(8,128)} %fusion.149, f32[2,4,512]{2,1,0:T(4,128)S(1)} %dynamic-slice_bitcast_fusion.3, bf16[2,2048,4,64]{1,3,2,0:T(8,128)(2,1)} %get-tuple-element.468, bf16[2,2,512,4,64]{2,4,3,1,0:T(8,128)(2,1)} %get-tuple-element.467, ...), kind=kOutput, calls=%fused_computation.15.clone.1 | convolution fusion | flops 1107292160 | bytes 69763072 | tf_op jit(solution)/shard_map/backward_attention/while/body/eval_jaxpr/cqhe,ckhe->chqk/dot_general | solution.py:183
  868.2 27.9 %multiply_convert_fusion.7 = bf16[2,4,512,2048]{3,2,1,0:T(8,128)(2,1)} fusion(f32[2,4,512,2048]{3,2,1,0:T(8,128)} %get-tuple-element.415, f32[2,4,512,2048]{3,2,1,0:T(8,128)} %fusion.149, f32[2,4,512]{2,1,0:T(4,128)S(1)} %get-tuple-element.416, f32[2,4,512]{2,1,0:T(4,128)S(1)} %dynamic-slice_bitcast_fusion.3), kind=kLoop, calls=%fused_computation.14.clone.1 | loop fusion | flops 41943040 | bytes 83918848 | tf_op jit(solution)/shard_map/backward_attention/while/body/eval_jaxpr/convert_element_type | solution.py:193
  896.2 9.7 fusion.150
  906.9 6.1 bitcast_add_fusion.4
  913.0 14.3 %fusion.149 = f32[2,4,512,2048]{3,2,1,0:T(8,128)} fusion(bf16[2,2048,4,64]{1,3,2,0:T(8,128)(2,1)S(1)} %get-tuple-element.465, bf16[2,2,512,4,64]{2,4,3,1,0:T(8,128)(2,1)} %get-tuple-element.464, s32[]{:T(128)S(6)} %copy.222), kind=kOutput, calls=%fused_computation.30.clone.1 | convolution fusion | flops 1073741824 | bytes 36175876 | tf_op jit(solution)/shard_map/backward_attention/while/body/eval_jaxpr/cqhe,ckhe->chqk/dot_general | solution.py:177
  927.3 17.2 %bitcast_add_fusion.5 = f32[2,2048,4,64]{1,3,2,0:T(8,128)} fusion(f32[2,2048,4,64]{1,3,2,0:T(8,128)} %get-tuple-element.451, f32[2,4,512,2048]{3,2,1,0:T(8,128)} %fusion.149, f32[2,4,512]{2,1,0:T(4,128)S(1)} %dynamic-slice_bitcast_fusion.3, pred[]{:T(512)S(6)} %compare.3, bf16[2,2,512,4,64]{2,4,3,1,0:T(8,128)(2,1)} %get-tuple-element.467, s32[]{:T(128)S(6)} %copy.222), kind=kOutput, calls=%fused_computation.21.clone.1 | convolution fusion | flops 1101004800 | bytes 42483716 | tf_op jit(solution)/shard_map/backward_attention/while/body/eval_jaxpr/chqk,cqhe->ckhe/dot_general | solution.py:186
  944.6 23.9 %multiply_reduce_fusion.6 = (f32[2,4,512]{2,1,0:T(4,128)S(1)}, f32[2,4,512,2048]{3,2,1,0:T(8,128)}) fusion(f32[2,4,512,2048]{3,2,1,0:T(8,128)} %fusion.149, f32[2,4,512]{2,1,0:T(4,128)S(1)} %dynamic-slice_bitcast_fusion.3, bf16[2,2048,4,64]{1,3,2,0:T(8,128)(2,1)} %get-tuple-element.468, bf16[2,2,512,4,64]{2,4,3,1,0:T(8,128)(2,1)} %get-tuple-element.467, ...), kind=kOutput, calls=%fused_computation.15.clone.1 | convolution fusion | flops 1107292160 | bytes 69763072 | tf_op jit(solution)/shard_map/backward_attention/while/body/eval_jaxpr/cqhe,ckhe->chqk/dot_general | solution.py:183
  968.4 27.9 %multiply_convert_fusion.7 = bf16[2,4,512,2048]{3,2,1,0:T(8,128)(2,1)} fusion(f32[2,4,512,2048]{3,2,1,0:T(8,128)} %get-tuple-element.415, f32[2,4,512,2048]{3,2,1,0:T(8,128)} %fusion.149, f32[2,4,512]{2,1,0:T(4,128)S(1)} %get-tuple-element.416, f32[2,4,512]{2,1,0:T(4,128)S(1)} %dynamic-slice_bitcast_fusion.3), kind=kLoop, calls=%fused_computation.14.clone.1 | loop fusion | flops 41943040 | bytes 83918848 | tf_op jit(solution)/shard_map/backward_attention/while/body/eval_jaxpr/convert_element_type | solution.py:193
  996.3 9.7 fusion.150
  1007.1 7.4 bitcast_add_fusion.4
  1025.2 11.2 bitcast_convert_fusion.1
  1036.4 10.1 bitcast_convert_fusion.2
  1056.7 7.7 bitcast_convert_fusion.3
  1064.5 11.8 convolution_convert_fusion.1
  1077.8 6.7 bitcast_convert_fusion
  1089.0 42.5 %reduce-scatter.27.cloned.1.call-done = bf16[128,1024]{1,0:T(8,128)(2,1)} async-done(((bf16[1024,1024]{1,0:T(8,128)(2,1)}), bf16[128,1024]{1,0:T(8,128)(2,1)}) %reduce-scatter.27.cloned.1.call-update) | async-done | bytes 262160 | tf_op jit(solution)/shard_map/weight_grads/reduce_scatter | solution.py:259
  1133.3 35.9 %reduce-scatter.25.cloned.1.call-done = bf16[128,256]{1,0:T(8,128)(2,1)} async-done(((bf16[1024,256]{1,0:T(8,128)(2,1)}), bf16[128,256]{1,0:T(8,128)(2,1)}) %reduce-scatter.25.cloned.1.call-update) | async-done | bytes 65552 | tf_op jit(solution)/shard_map/weight_grads/reduce_scatter | solution.py:259
  1170.7 40.0 %reduce-scatter.23.cloned.1.call-done = bf16[128,3,256]{2,0,1:T(8,128)(2,1)} async-done(((bf16[1024,3,256]{2,0,1:T(8,128)(2,1)}), bf16[128,3,256]{2,0,1:T(8,128)(2,1)}) %reduce-scatter.23.cloned.1.call-update) | async-done | bytes 196624 | tf_op jit(solution)/shard_map/weight_grads/reduce_scatter | solution.py:259
  1212.4 77.4 %reduce-scatter.13.cloned.1.call-done = bf16[2,256,1024]{2,1,0:T(8,128)(2,1)} async-done(((bf16[2,1024,1024]{2,1,0:T(8,128)(2,1)}), bf16[2,256,1024]{2,1,0:T(8,128)(2,1)}) %reduce-scatter.13.cloned.1.call-update) | async-done | bytes 1048592 | tf_op jit(solution)/shard_map/forward/reduce_scatter | solution.py:79
  1289.8 79.5 %reduce-scatter.21.cloned.1.call-done = bf16[2,256,1024]{2,1,0:T(8,128)(2,1)} async-done(((bf16[2,1024,1024]{2,1,0:T(8,128)(2,1)}), bf16[2,256,1024]{2,1,0:T(8,128)(2,1)}) %reduce-scatter.21.cloned.1.call-update) | async-done | bytes 1048592 | tf_op jit(solution)/shard_map/backward_attention/reduce_scatter | solution.py:79
  1369.4 5.7 fusion.74
  1397.4 9.5 all-gather.2
  (205 shorter events, 137.4 us)
Async XLA Ops:
  7.2 12.1 copy-start
  7.2 16.5 %copy-start.3 = (bf16[2,1,256,1024]{3,2,1,0:T(8,128)(2,1)S(1)}, bf16[2,1,256,1024]{3,2,1,0:T(8,128)(2,1)}, u32[]{:S(2)}) copy-start(bf16[2,1,256,1024]{3,2,1,0:T(8,128)(2,1)} %param.12) | copy-start | bytes 3145732
  7.2 67.7 %all-reduce.3.cloned.1.call-start = ((), (), s32[]{:S(2)}) async-start(), calls=%async_computation.31 | async-start | bytes 786432
  20.2 81.6 %all-gather.16.cloned.1.call-start = ((), (), s32[]{:S(2)}) async-start(), calls=%async_computation.13 | async-start | bytes 1769472 | tf_op jit(solution)/shard_map/weights/all_gather | solution.py:67
  23.7 161.0 %copy-start.26 = (f32[2,256]{1,0:T(2,128)}, f32[2,256]{1,0:T(2,128)S(1)}, u32[]{:S(2)}) copy-start(f32[2,256]{1,0:T(2,128)S(1)} %broadcast_multiply_fusion.5) | copy-start | bytes 6148
  77.0 10.2 all-to-all-start
  81.5 103.1 %all-gather.14.cloned.1.call-start = ((), (), s32[]{:S(2)}) async-start(), calls=%async_computation.12 | async-start | bytes 5242880 | tf_op jit(solution)/shard_map/forward/all_gather | solution.py:76
  81.6 103.1 %copy-start.33 = (f32[2,256]{1,0:T(2,128)}, f32[2,256]{1,0:T(2,128)S(1)}, u32[]{:S(2)}) copy-start(f32[2,256]{1,0:T(2,128)S(1)} %add_rsqrt_fusion.1) | copy-start | bytes 6148
  87.9 102.9 %copy-start.17 = (f32[2,1024]{1,0:T(2,128)}, f32[2,1024]{1,0:T(2,128)S(1)}, u32[]{:S(2)}) copy-start(f32[2,1024]{1,0:T(2,128)S(1)} %get-tuple-element.311) | copy-start | bytes 24580
  89.4 117.2 %all-gather.30.cloned.1.call-start = ((), (), s32[]{:S(2)}) async-start(), calls=%async_computation.30 | async-start | bytes 3145728 | tf_op jit(solution)/shard_map/forward/all_gather | solution.py:93
  192.4 22.4 %all-gather.28.cloned.1.call-start = ((), (), s32[]{:S(2)}) async-start(), calls=%async_computation.29 | async-start | bytes 3145728 | tf_op jit(solution)/shard_map/forward/all_gather | solution.py:92
  193.0 201.1 %reduce-scatter.11.cloned.1.call-start = ((), (), s32[]{:S(2)}) async-start(), calls=%async_computation.14 | async-start | bytes 5242880 | tf_op jit(solution)/shard_map/forward/reduce_scatter | solution.py:79
  316.0 78.2 %copy-start.12 = (f32[2,1024]{1,0:T(2,128)S(1)}, f32[2,1024]{1,0:T(2,128)}, u32[]{:S(2)}) copy-start(f32[2,1024]{1,0:T(2,128)} %get-tuple-element.312) | copy-start | bytes 24580
  316.0 82.3 %copy-start.14 = (f32[2,1024]{1,0:T(2,128)S(1)}, f32[2,1024]{1,0:T(2,128)}, u32[]{:S(2)}) copy-start(f32[2,1024]{1,0:T(2,128)} %get-tuple-element.309) | copy-start | bytes 24580
  316.0 82.3 %copy-start.32 = (f32[2,1024]{1,0:T(2,128)S(1)}, f32[2,1024]{1,0:T(2,128)}, u32[]{:S(2)}) copy-start(f32[2,1024]{1,0:T(2,128)} %get-tuple-element.308) | copy-start | bytes 24580
  316.0 108.3 %all-gather.20.cloned.1.call-start = ((), (), s32[]{:S(2)}) async-start(), calls=%async_computation.16 | async-start | bytes 2359296 | tf_op jit(solution)/shard_map/weights/all_gather | solution.py:67
  316.8 190.5 %all-gather.18.cloned.1.call-start = ((), (), s32[]{:S(2)}) async-start(), calls=%async_computation.15 | async-start | bytes 5242880 | tf_op jit(solution)/shard_map/forward/all_gather | solution.py:76
  396.2 320.6 %copy-start.19 = (f32[2,256]{1,0:T(2,128)}, f32[2,256]{1,0:T(2,128)S(1)}, u32[]{:S(2)}) copy-start(f32[2,256]{1,0:T(2,128)S(1)} %broadcast_multiply_fusion.4) | copy-start | bytes 6148
  398.3 318.4 %copy-start.21 = (f32[2,256]{1,0:T(2,128)}, f32[2,256]{1,0:T(2,128)S(1)}, u32[]{:S(2)}) copy-start(f32[2,256]{1,0:T(2,128)S(1)} %add_rsqrt_fusion) | copy-start | bytes 6148
  401.2 134.2 %all-gather.22.cloned.1.call-start = ((), (), s32[]{:S(2)}) async-start(), calls=%async_computation.17 | async-start | bytes 2359296 | tf_op jit(solution)/shard_map/weights/all_gather | solution.py:67
  402.0 215.7 %all-gather.24.cloned.1.call-start = ((), (), s32[]{:S(2)}) async-start(), calls=%async_computation.19 | async-start | bytes 5242880 | tf_op jit(solution)/shard_map/backward_ffn/all_gather | solution.py:76
  404.6 309.3 %reduce-scatter.15.cloned.1.call-start = ((), (), s32[]{:S(2)}) async-start(), calls=%async_computation.20 | async-start | bytes 5242880 | tf_op jit(solution)/shard_map/backward_ffn/reduce_scatter | solution.py:79
  617.6 14.5 %copy-start.35 = (bf16[1024,1024]{1,0:T(8,128)(2,1)S(1)}, bf16[1024,1024]{1,0:T(8,128)(2,1)}, u32[]{:S(2)}) copy-start(bf16[1024,1024]{1,0:T(8,128)(2,1)} %all-gather.20.cloned.1.call-done) | copy-start | bytes 6291460
  638.5 163.8 %all-gather.26.cloned.1.call-start = ((), (), s32[]{:S(2)}) async-start(), calls=%async_computation.21 | async-start | bytes 5242880 | tf_op jit(solution)/shard_map/backward_attention/all_gather | solution.py:76
  720.9 335.7 %reduce-scatter.17.cloned.1.call-start = ((), (), s32[]{:S(2)}) async-start(), calls=%async_computation.22 | async-start | bytes 3145728 | tf_op jit(solution)/shard_map/backward_attention/reduce_scatter | solution.py:215
  896.2 10.7 copy-start.2
  1020.0 36.7 %reduce-scatter.19.cloned.1.call-start = ((), (), s32[]{:S(2)}) async-start(), calls=%async_computation.23 | async-start | bytes 3145728 | tf_op jit(solution)/shard_map/backward_attention/reduce_scatter | solution.py:215
  1025.1 62.1 %reduce-scatter.29.cloned.1.call-start = ((), (), s32[]{:S(2)}) async-start(), calls=%async_computation.28 | async-start | bytes 2359296 | tf_op jit(solution)/shard_map/weight_grads/reduce_scatter | solution.py:259
  1036.4 95.1 %reduce-scatter.27.cloned.1.call-start = ((), (), s32[]{:S(2)}) async-start(), calls=%async_computation.27 | async-start | bytes 2359296 | tf_op jit(solution)/shard_map/weight_grads/reduce_scatter | solution.py:259
  1046.5 122.6 %reduce-scatter.25.cloned.1.call-start = ((), (), s32[]{:S(2)}) async-start(), calls=%async_computation.26 | async-start | bytes 589824 | tf_op jit(solution)/shard_map/weight_grads/reduce_scatter | solution.py:259
  1056.6 154.1 %reduce-scatter.23.cloned.1.call-start = ((), (), s32[]{:S(2)}) async-start(), calls=%async_computation.25 | async-start | bytes 1769472 | tf_op jit(solution)/shard_map/weight_grads/reduce_scatter | solution.py:259
  1064.5 225.4 %reduce-scatter.13.cloned.1.call-start = ((), (), s32[]{:S(2)}) async-start(), calls=%async_computation.18 | async-start | bytes 5242880 | tf_op jit(solution)/shard_map/forward/reduce_scatter | solution.py:79
  1076.3 293.0 %reduce-scatter.21.cloned.1.call-start = ((), (), s32[]{:S(2)}) async-start(), calls=%async_computation.24 | async-start | bytes 5242880 | tf_op jit(solution)/shard_map/backward_attention/reduce_scatter | solution.py:79
  1084.5 284.8 %copy-start.4 = (bf16[2,1,256,1024]{3,2,1,0:T(8,128)(2,1)S(1)}, bf16[2,1,256,1024]{3,2,1,0:T(8,128)(2,1)}, u32[]{:S(2)}) copy-start(bf16[2,1,256,1024]{3,2,1,0:T(8,128)(2,1)} %param.12) | copy-start | bytes 3145732
  1084.5 284.8 %copy-start.6 = (bf16[2,256,1024]{2,1,0:T(8,128)(2,1)S(1)}, bf16[2,256,1024]{2,1,0:T(8,128)(2,1)}, u32[]{:S(2)}) copy-start(bf16[2,256,1024]{2,1,0:T(8,128)(2,1)} %reduce-scatter.11.cloned.1.call-done) | copy-start | bytes 3145732
  1084.5 284.8 %copy-start.8 = (bf16[2,256,1024]{2,1,0:T(8,128)(2,1)S(1)}, bf16[2,256,1024]{2,1,0:T(8,128)(2,1)}, u32[]{:S(2)}) copy-start(bf16[2,256,1024]{2,1,0:T(8,128)(2,1)} %reduce-scatter.15.cloned.1.call-done) | copy-start | bytes 3145732
  1084.5 284.8 %copy-start.13 = (f32[2,1024]{1,0:T(2,128)S(1)}, f32[2,1024]{1,0:T(2,128)}, u32[]{:S(2)}) copy-start(f32[2,1024]{1,0:T(2,128)} %get-tuple-element.312) | copy-start | bytes 24580
  1084.5 284.8 %copy-start.15 = (f32[2,1024]{1,0:T(2,128)S(1)}, f32[2,1024]{1,0:T(2,128)}, u32[]{:S(2)}) copy-start(f32[2,1024]{1,0:T(2,128)} %get-tuple-element.309) | copy-start | bytes 24580
  1084.5 284.8 %copy-start.18 = (f32[2,1024]{1,0:T(2,128)S(1)}, f32[2,1024]{1,0:T(2,128)}, u32[]{:S(2)}) copy-start(f32[2,1024]{1,0:T(2,128)} %copy-done.17) | copy-start | bytes 24580
  1084.5 284.8 %copy-start.20 = (f32[2,256]{1,0:T(2,128)S(1)}, f32[2,256]{1,0:T(2,128)}, u32[]{:S(2)}) copy-start(f32[2,256]{1,0:T(2,128)} %copy-done.19) | copy-start | bytes 6148
  1084.5 284.8 %copy-start.22 = (f32[2,256]{1,0:T(2,128)S(1)}, f32[2,256]{1,0:T(2,128)}, u32[]{:S(2)}) copy-start(f32[2,256]{1,0:T(2,128)} %copy-done.21) | copy-start | bytes 6148
  1084.5 284.8 %copy-start.24 = (f32[2,1024]{1,0:T(2,128)S(1)}, f32[2,1024]{1,0:T(2,128)}, u32[]{:S(2)}) copy-start(f32[2,1024]{1,0:T(2,128)} %get-tuple-element.307) | copy-start | bytes 24580
  1084.5 284.8 %copy-start.27 = (f32[2,256]{1,0:T(2,128)S(1)}, f32[2,256]{1,0:T(2,128)}, u32[]{:S(2)}) copy-start(f32[2,256]{1,0:T(2,128)} %copy-done.26) | copy-start | bytes 6148
  1084.6 284.8 %copy-start.29 = (f32[2,256]{1,0:T(2,128)S(1)}, f32[2,256]{1,0:T(2,128)}, u32[]{:S(2)}) copy-start(f32[2,256]{1,0:T(2,128)} %copy-done.28) | copy-start | bytes 6148
  1084.6 284.8 %copy-start.31 = (f32[2,256]{1,0:T(2,128)S(1)}, f32[2,256]{1,0:T(2,128)}, u32[]{:S(2)}) copy-start(f32[2,256]{1,0:T(2,128)} %copy-done.30) | copy-start | bytes 6148
  1084.6 284.8 %copy-start.34 = (f32[2,256]{1,0:T(2,128)S(1)}, f32[2,256]{1,0:T(2,128)}, u32[]{:S(2)}) copy-start(f32[2,256]{1,0:T(2,128)} %copy-done.33) | copy-start | bytes 6148
  1383.3 10.0 all-to-all-start.1
  1387.5 21.7 %copy-start.1 = (bf16[128,6,256]{2,0,1:T(8,128)(2,1)S(1)}, bf16[128,6,256]{2,0,1:T(8,128)(2,1)}, u32[]{:S(2)}) copy-start(bf16[128,6,256]{2,0,1:T(8,128)(2,1)} %param.19) | copy-start | bytes 1179652
  (14 other events, 55.6 us)
Sparse Core Ops, SparseCore 0:
  20.3 54.5 all-reduce.2
  76.8 24.9 all-gather.15
  103.9 80.7 all-gather.13
  192.5 9.1 all-gather.29
  203.1 11.7 all-gather.27
  316.1 77.9 reduce-scatter.10
  396.0 28.2 all-gather.19
  426.5 80.7 all-gather.17
  509.1 26.2 all-gather.21
  536.9 80.7 all-gather.23
  638.6 75.2 reduce-scatter.14
  721.0 81.2 all-gather.25
  1020.1 8.3 reduce-scatter.16
  1030.6 11.0 reduce-scatter.18
  1044.8 42.3 reduce-scatter.28
  1090.3 41.1 reduce-scatter.26
  1135.0 34.1 reduce-scatter.24
  1172.3 38.3 reduce-scatter.22
  1213.0 76.7 reduce-scatter.12
  1292.0 77.2 reduce-scatter.20
where the time goes:
time: 1420 us
  waiting for transfers between devices  874 us (62%)
  matrix products  302 us (21%)
  other arithmetic  129 us (9%)
  local copies, waits for them, and re-layouts  53.9 us (4%)
  blocking collectives  31.3 us (2%)
  between operations  15.2 us (1%)
    all_gather x4, waiting for transfers between devices, gather_tokens(): return lax.all_gather(values, 'tensor', axis=1, tiled=True)  329 us
    reduce_scatter x4, waiting for transfers between devices, scatter_tokens(): lax.psum_scatter(values.astype(jnp.bfloat16), 'tensor', scatter_dimension...  309 us
    reduce_scatter x4, waiting for transfers between devices, on_device(): lax.psum_scatter(total.astype(jnp.bfloat16), ('dp', 'frame'), scatter_dim...  121 us
    convert_element_type x2, other arithmetic, attend_back(): grad_scores = (probs * (grad_probs - row_terms)).astype(jnp.bfloat16)  55.8 us
    unnamed x21, waiting for transfers between devices  53.7 us
    all_gather x3, waiting for transfers between devices, on_device(): lax.all_gather(w, ('dp', 'frame'), axis=0, tiled=True)  49.6 us
    dot_general x2, matrix products, attend_back(): jnp.einsum('cqhe,ckhe->chqk', grad_block, value_heads, preferred_element_...  47.7 us
    dot_general x2, matrix products, attend_back(): jnp.einsum('chqk,cqhe->ckhe', probs.astype(jnp.bfloat16), grad_block, pre...  33.3 us
  transfers between devices with their start and end apart: 22, of which 19 were waited for; matrix products, arithmetic and copies ran while one was open for 8% of the time, Pallas kernels for 0%

commit v1 on v0

--- a/solution.py
+++ b/solution.py
@@ -7,6 +7,18 @@
 HEAD_DIM = 64
 epsilon = 1e-06
 highest = lax.Precision.HIGHEST
+
+
+def ring_gather(value, axis, dim):
+    ways, here, step = (lax.axis_size(axis), lax.axis_index(axis), value.shape[dim])
+    dims = [n * ways if d == dim else n for d, n in enumerate(value.shape)]
+    full = lax.dynamic_update_slice_in_dim(
+        jnp.zeros(dims, value.dtype), value, here * step, axis=dim
+    )
+    for far in range(1, ways):
+        value = lax.ppermute(value, axis, [(d, (d + 1) % ways) for d in range(ways)])
+        full = lax.dynamic_update_slice_in_dim(full, value, (here - far) % ways * step, axis=dim)
+    return full
 
 
 def normalize(values):
@@ -64,7 +76,7 @@
         modulation = modulation.reshape(clips, 6, 1, model_width)
     with jax.named_scope("weights"):
         joint_weight, mixer_weight, upward_weight, downward_weight = (
-            lax.all_gather(w, ("dp", "frame"), axis=0, tiled=True)
+            ring_gather(w, ("dp", "frame"), 0)
             for w in (qkv_weight, out_weight, up_weight, down_weight)
         )
     residual = tokens[:, 0].astype(jnp.float32)

time: 1420 us -> 1370 us (0.965)
  waiting for transfers between devices: 874 us -> 812 us
  local copies, waits for them, and re-layouts: 53.9 us -> 68.8 us
    all_gather x4, waiting for transfers between devices: 329 us -> 215 us  [gather_tokens(): return lax.all_gather(values, 'tensor', axis=1, tiled=True)]
    ppermute x0 -> x28, waiting for transfers between devices: none -> 108 us  [ring_gather(): lax.ppermute(value, axis, [(d, (d + 1) % ways) for d in range(ways)])]
    all_gather x3 -> x0, waiting for transfers between devices: 49.6 us -> none  [on_device(): lax.all_gather(w, ('dp', 'frame'), axis=0, tiled=True)]
    unnamed x21 -> x18, waiting for transfers between devices: 53.7 us -> 54.2 us
  transfers between devices with their start and end apart: 22 -> 47, of which waited for: 19 -> 42; matrix products, arithmetic and copies ran while one was open for 8% -> 8% of each run, Pallas kernels for 0% -> 0%
where the time goes in v1:
time: 1370 us; the launch traced here: 1360 us
  waiting for transfers between devices  812 us (59%)
  matrix products  302 us (22%)
  other arithmetic  126 us (9%)
  local copies, waits for them, and re-layouts  68.8 us (5%)
  blocking collectives  20.2 us (1%)
  between operations  15 us (1%)
    reduce_scatter x4, waiting for transfers between devices, scatter_tokens(): lax.psum_scatter(values.astype(jnp.bfloat16), 'tensor', scatter_dimension...  306 us
    all_gather x4, waiting for transfers between devices, gather_tokens(): return lax.all_gather(values, 'tensor', axis=1, tiled=True)  215 us
    reduce_scatter x4, waiting for transfers between devices, on_device(): lax.psum_scatter(total.astype(jnp.bfloat16), ('dp', 'frame'), scatter_dim...  122 us
    ppermute x28, waiting for transfers between devices, ring_gather(): lax.ppermute(value, axis, [(d, (d + 1) % ways) for d in range(ways)])  108 us
    convert_element_type x2, other arithmetic, attend_back(): grad_scores = (probs * (grad_probs - row_terms)).astype(jnp.bfloat16)  55.8 us
    unnamed x18, waiting for transfers between devices  54.2 us
    dot_general x2, matrix products, attend_back(): jnp.einsum('cqhe,ckhe->chqk', grad_block, value_heads, preferred_element_...  47.7 us
    dot_general x2, matrix products, attend_back(): jnp.einsum('chqk,cqhe->ckhe', probs.astype(jnp.bfloat16), grad_block, pre...  33.3 us
  transfers between devices with their start and end apart: 47, of which 42 were waited for; matrix products, arithmetic and copies ran while one was open for 8% of the time, Pallas kernels for 0%

profile of v1, /device:TPU:0, one launch (start us, length us, event | category | flops | bytes accessed | tf_op | source)
XLA Modules:
  0.0 1357.4 jit_solution(7343074640658983733)
XLA Ops:
  7.3 10.7 all-gather.3
  21.5 53.5 %all-reduce.3.cloned.1.call-done = f32[8,2,4,6,256]{4,2,3,1,0:T(4,128)} async-done(((f32[8,2,4,6,256]{4,2,3,1,0:T(4,128)}), f32[8,2,4,6,256]{4,2,3,1,0:T(4,128)}) %all-reduce.3.cloned.1.call-update) | async-done | bytes 393232
  89.6 6.0 collective-permute-done
  95.6 6.0 collective-permute-done.1
  101.6 6.0 collective-permute-done.2
  113.6 5.9 collective-permute-done.4
  119.6 5.9 collective-permute-done.5
  125.6 5.9 collective-permute-done.6
  131.6 35.7 %all-gather.11.cloned.1.call-done = bf16[2,1024,1024]{2,1,0:T(8,128)(2,1)} async-done(((bf16[2,256,1024]{2,1,0:T(8,128)(2,1)}), bf16[2,1024,1024]{2,1,0:T(8,128)(2,1)}) %all-gather.11.cloned.1.call-update) | async-done | bytes 4194320 | tf_op jit(solution)/shard_map/forward/all_gather | solution.py:88
  217.8 87.8 %while.27 = (s32[]{:T(128)}, bf16[2,2,512,4,64]{2,4,3,1,0:T(8,128)(2,1)}, f32[2,2,4,512]{3,2,1,0:T(4,128)S(1)}, bf16[2,2,512,4,64]{2,4,3,1,0:T(8,128)(2,1)}, bf1...) while((s32[]{:T(128)}, bf16[2,2,512,4,64]{2,4,3,1,0:T(8,128)(2,1)}, ...), condition=%wide.region_6.7_spmd, body=%wide.region_3.6_spmd.sunk | while | flops 2223239168 | bytes 106037344 | solution.py:130
  217.8 14.3 %multiply_reduce_fusion.5 = (f32[2,4,512]{2,1,0:T(4,128)S(1)}, f32[2,4,512,2048]{3,2,1,0:T(8,128)}) fusion(bf16[2,2048,4,64]{1,3,2,0:T(8,128)(2,1)S(1)} %get-tuple-element.435, bf16[2,2,512,4,64]{2,4,3,1,0:T(8,128)(2,1)} %get-tuple-element.434, s32[]{:T(128)S(6)} %copy.220), kind=kOutput, calls=%fused_computation.2.clone.1 | convolution fusion | flops 1090514944 | bytes 36192260 | tf_op jit(solution)/shard_map/forward/while/body/eval_jaxpr/cqhe,ckhe->chqk/dot_general | solution.py:116
  232.1 14.0 %fusion.138 = f32[2,4,512]{2,1,0:T(4,128)S(1)} fusion(f32[2,4,512,2048]{3,2,1,0:T(8,128)} %get-tuple-element.404, f32[2,4,512]{2,1,0:T(4,128)S(1)} %get-tuple-element.405), kind=kLoop, calls=%fused_computation.3.clone.1 | loop fusion | flops 25161728 | bytes 33587200 | tf_op jit(solution)/shard_map/forward/while/body/eval_jaxpr/reduce_sum | solution.py:123
  246.2 15.5 %fusion.139 = bf16[2,2,512,4,64]{2,4,3,1,0:T(8,128)(2,1)} fusion(bf16[2,2,512,4,64]{2,4,3,1,0:T(8,128)(2,1)} %get-tuple-element.425, s32[]{:T(128)S(6)} %copy.220, bf16[2,2048,4,64]{1,3,2,0:T(8,128)(2,1)} %get-tuple-element.436, f32[2,4,512,2048]{3,2,1,0:T(8,128)} %get-tuple-element.404, f32[2,4,512]{2,1,0:T(4,128)S(1)} %fusion.138, ...), kind=kOutput, calls=%fused_computation.7.clone.1 | convolution fusion | flops 1107558400 | bytes 36208644 | tf_op jit(solution)/shard_map/forward/while/body/eval_jaxpr/chqk,ckhe->cqhe/dot_general | solution.py:125
  261.7 14.3 %multiply_reduce_fusion.5 = (f32[2,4,512]{2,1,0:T(4,128)S(1)}, f32[2,4,512,2048]{3,2,1,0:T(8,128)}) fusion(bf16[2,2048,4,64]{1,3,2,0:T(8,128)(2,1)S(1)} %get-tuple-element.435, bf16[2,2,512,4,64]{2,4,3,1,0:T(8,128)(2,1)} %get-tuple-element.434, s32[]{:T(128)S(6)} %copy.220), kind=kOutput, calls=%fused_computation.2.clone.1 | convolution fusion | flops 1090514944 | bytes 36192260 | tf_op jit(solution)/shard_map/forward/while/body/eval_jaxpr/cqhe,ckhe->chqk/dot_general | solution.py:116
  276.1 14.0 %fusion.138 = f32[2,4,512]{2,1,0:T(4,128)S(1)} fusion(f32[2,4,512,2048]{3,2,1,0:T(8,128)} %get-tuple-element.404, f32[2,4,512]{2,1,0:T(4,128)S(1)} %get-tuple-element.405), kind=kLoop, calls=%fused_computation.3.clone.1 | loop fusion | flops 25161728 | bytes 33587200 | tf_op jit(solution)/shard_map/forward/while/body/eval_jaxpr/reduce_sum | solution.py:123
  290.1 15.5 %fusion.139 = bf16[2,2,512,4,64]{2,4,3,1,0:T(8,128)(2,1)} fusion(bf16[2,2,512,4,64]{2,4,3,1,0:T(8,128)(2,1)} %get-tuple-element.425, s32[]{:T(128)S(6)} %copy.220, bf16[2,2048,4,64]{1,3,2,0:T(8,128)(2,1)} %get-tuple-element.436, f32[2,4,512,2048]{3,2,1,0:T(8,128)} %get-tuple-element.404, f32[2,4,512]{2,1,0:T(4,128)S(1)} %fusion.138, ...), kind=kOutput, calls=%fused_computation.7.clone.1 | convolution fusion | flops 1107558400 | bytes 36208644 | tf_op jit(solution)/shard_map/forward/while/body/eval_jaxpr/chqk,ckhe->cqhe/dot_general | solution.py:125
  316.5 74.1 %reduce-scatter.11.cloned.1.call-done = bf16[2,256,1024]{2,1,0:T(8,128)(2,1)} async-done(((bf16[2,1024,1024]{2,1,0:T(8,128)(2,1)}), bf16[2,256,1024]{2,1,0:T(8,128)(2,1)}) %reduce-scatter.11.cloned.1.call-update) | async-done | bytes 1048592 | tf_op jit(solution)/shard_map/forward/reduce_scatter | solution.py:91
  450.1 27.5 %all-gather.13.cloned.1.call-done = bf16[2,1024,1024]{2,1,0:T(8,128)(2,1)} async-done(((bf16[2,256,1024]{2,1,0:T(8,128)(2,1)}), bf16[2,1024,1024]{2,1,0:T(8,128)(2,1)}) %all-gather.13.cloned.1.call-update) | async-done | bytes 4194320 | tf_op jit(solution)/shard_map/forward/all_gather | solution.py:88
  477.7 10.8 fusion.81
  488.5 70.0 %all-gather.15.cloned.1.call-done = bf16[2,1024,1024]{2,1,0:T(8,128)(2,1)} async-done(((bf16[2,256,1024]{2,1,0:T(8,128)(2,1)}), bf16[2,1024,1024]{2,1,0:T(8,128)(2,1)}) %all-gather.15.cloned.1.call-update) | async-done | bytes 4194320 | tf_op jit(solution)/shard_map/backward_ffn/all_gather | solution.py:88
  558.5 12.4 fusion.40
  572.9 7.7 convolution_convert_fusion
  580.9 75.2 %reduce-scatter.15.cloned.1.call-done = bf16[2,256,1024]{2,1,0:T(8,128)(2,1)} async-done(((bf16[2,1024,1024]{2,1,0:T(8,128)(2,1)}), bf16[2,256,1024]{2,1,0:T(8,128)(2,1)}) %reduce-scatter.15.cloned.1.call-update) | async-done | bytes 1048592 | tf_op jit(solution)/shard_map/backward_ffn/reduce_scatter | solution.py:91
  663.1 81.3 %all-gather.17.cloned.1.call-done = bf16[2,1024,1024]{2,1,0:T(8,128)(2,1)} async-done(((bf16[2,256,1024]{2,1,0:T(8,128)(2,1)}), bf16[2,1024,1024]{2,1,0:T(8,128)(2,1)}) %all-gather.17.cloned.1.call-update) | async-done | bytes 4194320 | tf_op jit(solution)/shard_map/backward_attention/all_gather | solution.py:88
  756.3 200.8 %while.28 = (s32[]{:T(128)}, f32[2,2048,4,64]{1,3,2,0:T(8,128)}, f32[2,2048,4,64]{1,3,2,0:T(8,128)}, bf16[2,2,512,4,64]{2,4,3,1,0:T(8,128)(2,1)}, bf16[2,2,512,4...) while((s32[]{:T(128)}, f32[2,2048,4,64]{1,3,2,0:T(8,128)}, ...), condition=%wide.region_16.17_spmd.clone, body=%wide.region_14.16_spmd.clone.sunk | while | flops 5474873344 | bytes 345096384 | solution.py:222
  756.3 14.3 %fusion.149 = f32[2,4,512,2048]{3,2,1,0:T(8,128)} fusion(bf16[2,2048,4,64]{1,3,2,0:T(8,128)(2,1)S(1)} %get-tuple-element.465, bf16[2,2,512,4,64]{2,4,3,1,0:T(8,128)(2,1)} %get-tuple-element.464, s32[]{:T(128)S(6)} %copy.254), kind=kOutput, calls=%fused_computation.30.clone.1 | convolution fusion | flops 1073741824 | bytes 36175876 | tf_op jit(solution)/shard_map/backward_attention/while/body/eval_jaxpr/cqhe,ckhe->chqk/dot_general | solution.py:189
  770.5 16.0 %bitcast_add_fusion.5 = f32[2,2048,4,64]{1,3,2,0:T(8,128)} fusion(f32[2,2048,4,64]{1,3,2,0:T(8,128)} %get-tuple-element.451, f32[2,4,512,2048]{3,2,1,0:T(8,128)} %fusion.149, f32[2,4,512]{2,1,0:T(4,128)S(1)} %dynamic-slice_bitcast_fusion.3, pred[]{:T(512)S(6)} %compare.10, bf16[2,2,512,4,64]{2,4,3,1,0:T(8,128)(2,1)} %get-tuple-element.467, ...), kind=kOutput, calls=%fused_computation.21.clone.1 | convolution fusion | flops 1101004800 | bytes 42483716 | tf_op jit(solution)/shard_map/backward_attention/while/body/eval_jaxpr/chqk,cqhe->ckhe/dot_general | solution.py:198
  786.6 23.9 %multiply_reduce_fusion.6 = (f32[2,4,512]{2,1,0:T(4,128)S(1)}, f32[2,4,512,2048]{3,2,1,0:T(8,128)}) fusion(f32[2,4,512,2048]{3,2,1,0:T(8,128)} %fusion.149, f32[2,4,512]{2,1,0:T(4,128)S(1)} %dynamic-slice_bitcast_fusion.3, bf16[2,2048,4,64]{1,3,2,0:T(8,128)(2,1)} %get-tuple-element.468, bf16[2,2,512,4,64]{2,4,3,1,0:T(8,128)(2,1)} %get-tuple-element.467, ...), kind=kOutput, calls=%fused_computation.15.clone.1 | convolution fusion | flops 1107292160 | bytes 69763072 | tf_op jit(solution)/shard_map/backward_attention/while/body/eval_jaxpr/cqhe,ckhe->chqk/dot_general | solution.py:195
  810.5 27.9 %multiply_convert_fusion.7 = bf16[2,4,512,2048]{3,2,1,0:T(8,128)(2,1)} fusion(f32[2,4,512,2048]{3,2,1,0:T(8,128)} %get-tuple-element.415, f32[2,4,512,2048]{3,2,1,0:T(8,128)} %fusion.149, f32[2,4,512]{2,1,0:T(4,128)S(1)} %get-tuple-element.416, f32[2,4,512]{2,1,0:T(4,128)S(1)} %dynamic-slice_bitcast_fusion.3), kind=kLoop, calls=%fused_computation.14.clone.1 | loop fusion | flops 41943040 | bytes 83918848 | tf_op jit(solution)/shard_map/backward_attention/while/body/eval_jaxpr/convert_element_type | solution.py:205
  838.4 9.7 fusion.150
  849.1 6.2 bitcast_add_fusion.4
  855.3 14.3 %fusion.149 = f32[2,4,512,2048]{3,2,1,0:T(8,128)} fusion(bf16[2,2048,4,64]{1,3,2,0:T(8,128)(2,1)S(1)} %get-tuple-element.465, bf16[2,2,512,4,64]{2,4,3,1,0:T(8,128)(2,1)} %get-tuple-element.464, s32[]{:T(128)S(6)} %copy.254), kind=kOutput, calls=%fused_computation.30.clone.1 | convolution fusion | flops 1073741824 | bytes 36175876 | tf_op jit(solution)/shard_map/backward_attention/while/body/eval_jaxpr/cqhe,ckhe->chqk/dot_general | solution.py:189
  869.6 17.2 %bitcast_add_fusion.5 = f32[2,2048,4,64]{1,3,2,0:T(8,128)} fusion(f32[2,2048,4,64]{1,3,2,0:T(8,128)} %get-tuple-element.451, f32[2,4,512,2048]{3,2,1,0:T(8,128)} %fusion.149, f32[2,4,512]{2,1,0:T(4,128)S(1)} %dynamic-slice_bitcast_fusion.3, pred[]{:T(512)S(6)} %compare.10, bf16[2,2,512,4,64]{2,4,3,1,0:T(8,128)(2,1)} %get-tuple-element.467, ...), kind=kOutput, calls=%fused_computation.21.clone.1 | convolution fusion | flops 1101004800 | bytes 42483716 | tf_op jit(solution)/shard_map/backward_attention/while/body/eval_jaxpr/chqk,cqhe->ckhe/dot_general | solution.py:198
  886.8 23.8 %multiply_reduce_fusion.6 = (f32[2,4,512]{2,1,0:T(4,128)S(1)}, f32[2,4,512,2048]{3,2,1,0:T(8,128)}) fusion(f32[2,4,512,2048]{3,2,1,0:T(8,128)} %fusion.149, f32[2,4,512]{2,1,0:T(4,128)S(1)} %dynamic-slice_bitcast_fusion.3, bf16[2,2048,4,64]{1,3,2,0:T(8,128)(2,1)} %get-tuple-element.468, bf16[2,2,512,4,64]{2,4,3,1,0:T(8,128)(2,1)} %get-tuple-element.467, ...), kind=kOutput, calls=%fused_computation.15.clone.1 | convolution fusion | flops 1107292160 | bytes 69763072 | tf_op jit(solution)/shard_map/backward_attention/while/body/eval_jaxpr/cqhe,ckhe->chqk/dot_general | solution.py:195
  910.6 27.9 %multiply_convert_fusion.7 = bf16[2,4,512,2048]{3,2,1,0:T(8,128)(2,1)} fusion(f32[2,4,512,2048]{3,2,1,0:T(8,128)} %get-tuple-element.415, f32[2,4,512,2048]{3,2,1,0:T(8,128)} %fusion.149, f32[2,4,512]{2,1,0:T(4,128)S(1)} %get-tuple-element.416, f32[2,4,512]{2,1,0:T(4,128)S(1)} %dynamic-slice_bitcast_fusion.3), kind=kLoop, calls=%fused_computation.14.clone.1 | loop fusion | flops 41943040 | bytes 83918848 | tf_op jit(solution)/shard_map/backward_attention/while/body/eval_jaxpr/convert_element_type | solution.py:205
  938.5 9.7 fusion.150
  949.2 7.5 bitcast_add_fusion.4
  967.3 11.1 bitcast_convert_fusion.1
  978.5 10.1 bitcast_convert_fusion.2
  998.2 7.7 bitcast_convert_fusion.3
  1006.0 11.8 convolution_convert_fusion.1
  1019.2 6.9 bitcast_convert_fusion
  1031.2 42.6 %reduce-scatter.27.cloned.1.call-done = bf16[128,1024]{1,0:T(8,128)(2,1)} async-done(((bf16[1024,1024]{1,0:T(8,128)(2,1)}), bf16[128,1024]{1,0:T(8,128)(2,1)}) %reduce-scatter.27.cloned.1.call-update) | async-done | bytes 262160 | tf_op jit(solution)/shard_map/weight_grads/reduce_scatter | solution.py:271
  1075.6 35.9 %reduce-scatter.25.cloned.1.call-done = bf16[128,256]{1,0:T(8,128)(2,1)} async-done(((bf16[1024,256]{1,0:T(8,128)(2,1)}), bf16[128,256]{1,0:T(8,128)(2,1)}) %reduce-scatter.25.cloned.1.call-update) | async-done | bytes 65552 | tf_op jit(solution)/shard_map/weight_grads/reduce_scatter | solution.py:271
  1113.0 40.0 %reduce-scatter.23.cloned.1.call-done = bf16[128,3,256]{2,0,1:T(8,128)(2,1)} async-done(((bf16[1024,3,256]{2,0,1:T(8,128)(2,1)}), bf16[128,3,256]{2,0,1:T(8,128)(2,1)}) %reduce-scatter.23.cloned.1.call-update) | async-done | bytes 196624 | tf_op jit(solution)/shard_map/weight_grads/reduce_scatter | solution.py:271
  1154.7 77.3 %reduce-scatter.13.cloned.1.call-done = bf16[2,256,1024]{2,1,0:T(8,128)(2,1)} async-done(((bf16[2,1024,1024]{2,1,0:T(8,128)(2,1)}), bf16[2,256,1024]{2,1,0:T(8,128)(2,1)}) %reduce-scatter.13.cloned.1.call-update) | async-done | bytes 1048592 | tf_op jit(solution)/shard_map/forward/reduce_scatter | solution.py:91
  1232.0 79.5 %reduce-scatter.21.cloned.1.call-done = bf16[2,256,1024]{2,1,0:T(8,128)(2,1)} async-done(((bf16[2,1024,1024]{2,1,0:T(8,128)(2,1)}), bf16[2,256,1024]{2,1,0:T(8,128)(2,1)}) %reduce-scatter.21.cloned.1.call-update) | async-done | bytes 1048592 | tf_op jit(solution)/shard_map/backward_attention/reduce_scatter | solution.py:91
  1339.6 9.5 all-gather.2
  (301 shorter events, 228.6 us)
Async XLA Ops:
  7.2 67.7 %all-reduce.3.cloned.1.call-start = ((), (), s32[]{:S(2)}) async-start(), calls=%async_computation.28 | async-start | bytes 786432
  77.0 10.2 all-to-all-start
  81.6 85.6 %all-gather.11.cloned.1.call-start = ((), (), s32[]{:S(2)}) async-start(), calls=%async_computation.12 | async-start | bytes 5242880 | tf_op jit(solution)/shard_map/forward/all_gather | solution.py:88
  89.5 121.4 %all-gather.21.cloned.1.call-start = ((), (), s32[]{:S(2)}) async-start(), calls=%async_computation.27 | async-start | bytes 3145728 | tf_op jit(solution)/shard_map/forward/all_gather | solution.py:105
  89.5 6.0 collective-permute-start
  95.6 6.0 collective-permute-start.1
  101.6 6.0 collective-permute-start.2
  107.6 6.0 collective-permute-start.3
  113.5 6.0 collective-permute-start.4
  119.5 6.0 collective-permute-start.5
  125.5 6.0 collective-permute-start.6
  174.4 40.5 %all-gather.19.cloned.1.call-start = ((), (), s32[]{:S(2)}) async-start(), calls=%async_computation.26 | async-start | bytes 3145728 | tf_op jit(solution)/shard_map/forward/all_gather | solution.py:104
  175.0 215.6 %reduce-scatter.11.cloned.1.call-start = ((), (), s32[]{:S(2)}) async-start(), calls=%async_computation.13 | async-start | bytes 5242880 | tf_op jit(solution)/shard_map/forward/reduce_scatter | solution.py:91
  175.2 4.6 collective-permute-start.7
  179.8 4.6 collective-permute-start.8
  184.4 4.6 collective-permute-start.9
  189.0 4.6 collective-permute-start.10
  193.6 4.6 collective-permute-start.11
  198.2 4.6 collective-permute-start.12
  202.8 4.7 collective-permute-start.13
  316.1 161.6 %all-gather.13.cloned.1.call-start = ((), (), s32[]{:S(2)}) async-start(), calls=%async_computation.14 | async-start | bytes 5242880 | tf_op jit(solution)/shard_map/forward/all_gather | solution.py:88
  396.3 162.2 %all-gather.15.cloned.1.call-start = ((), (), s32[]{:S(2)}) async-start(), calls=%async_computation.16 | async-start | bytes 5242880 | tf_op jit(solution)/shard_map/backward_ffn/all_gather | solution.py:88
  398.9 257.2 %reduce-scatter.15.cloned.1.call-start = ((), (), s32[]{:S(2)}) async-start(), calls=%async_computation.17 | async-start | bytes 5242880 | tf_op jit(solution)/shard_map/backward_ffn/reduce_scatter | solution.py:91
  398.9 6.7 collective-permute-start.14
  399.0 9.5 collective-permute-start.21
  405.7 6.7 collective-permute-start.15
  408.5 6.7 collective-permute-start.22
  412.4 7.5 collective-permute-start.16
  415.2 6.7 collective-permute-start.23
  419.8 6.7 collective-permute-start.17
  421.9 7.5 collective-permute-start.24
  426.5 6.7 collective-permute-start.18
  429.3 6.7 collective-permute-start.25
  433.2 6.7 collective-permute-start.19
  436.0 6.7 collective-permute-start.26
  439.9 6.7 collective-permute-start.20
  442.7 6.7 collective-permute-start.27
  580.6 163.8 %all-gather.17.cloned.1.call-start = ((), (), s32[]{:S(2)}) async-start(), calls=%async_computation.18 | async-start | bytes 5242880 | tf_op jit(solution)/shard_map/backward_attention/all_gather | solution.py:88
  663.1 335.1 %reduce-scatter.17.cloned.1.call-start = ((), (), s32[]{:S(2)}) async-start(), calls=%async_computation.19 | async-start | bytes 3145728 | tf_op jit(solution)/shard_map/backward_attention/reduce_scatter | solution.py:227
  962.2 36.0 %reduce-scatter.19.cloned.1.call-start = ((), (), s32[]{:S(2)}) async-start(), calls=%async_computation.20 | async-start | bytes 3145728 | tf_op jit(solution)/shard_map/backward_attention/reduce_scatter | solution.py:227
  967.3 62.2 %reduce-scatter.29.cloned.1.call-start = ((), (), s32[]{:S(2)}) async-start(), calls=%async_computation.25 | async-start | bytes 2359296 | tf_op jit(solution)/shard_map/weight_grads/reduce_scatter | solution.py:271
  978.5 95.4 %reduce-scatter.27.cloned.1.call-start = ((), (), s32[]{:S(2)}) async-start(), calls=%async_computation.24 | async-start | bytes 2359296 | tf_op jit(solution)/shard_map/weight_grads/reduce_scatter | solution.py:271
  988.6 122.8 %reduce-scatter.25.cloned.1.call-start = ((), (), s32[]{:S(2)}) async-start(), calls=%async_computation.23 | async-start | bytes 589824 | tf_op jit(solution)/shard_map/weight_grads/reduce_scatter | solution.py:271
  998.1 154.9 %reduce-scatter.23.cloned.1.call-start = ((), (), s32[]{:S(2)}) async-start(), calls=%async_computation.22 | async-start | bytes 1769472 | tf_op jit(solution)/shard_map/weight_grads/reduce_scatter | solution.py:271
  1006.0 226.0 %reduce-scatter.13.cloned.1.call-start = ((), (), s32[]{:S(2)}) async-start(), calls=%async_computation.15 | async-start | bytes 5242880 | tf_op jit(solution)/shard_map/forward/reduce_scatter | solution.py:91
  1017.8 293.6 %reduce-scatter.21.cloned.1.call-start = ((), (), s32[]{:S(2)}) async-start(), calls=%async_computation.21 | async-start | bytes 5242880 | tf_op jit(solution)/shard_map/backward_attention/reduce_scatter | solution.py:91
  1026.2 285.3 %copy-start.9 = (bf16[2,256,1024]{2,1,0:T(8,128)(2,1)S(1)}, bf16[2,256,1024]{2,1,0:T(8,128)(2,1)}, u32[]{:S(2)}) copy-start(bf16[2,256,1024]{2,1,0:T(8,128)(2,1)} %reduce-scatter.15.cloned.1.call-done) | copy-start | bytes 3145732
  1325.5 10.0 all-to-all-start.1
  (46 other events, 4358.4 us)
Sparse Core Ops, SparseCore 0:
  20.4 54.5 all-reduce.2
  89.5 77.6 all-gather.10
  174.5 9.0 all-gather.20
  185.0 11.7 all-gather.18
  316.2 74.3 reduce-scatter.10
  396.4 81.2 all-gather.12
  479.2 79.2 all-gather.14
  580.7 75.2 reduce-scatter.14
  663.2 81.2 all-gather.16
  962.3 8.2 reduce-scatter.16
  972.8 11.0 reduce-scatter.18
  987.0 42.3 reduce-scatter.28
  1032.7 41.0 reduce-scatter.26
  1077.3 34.0 reduce-scatter.24
  1114.6 38.3 reduce-scatter.22
  1155.2 76.7 reduce-scatter.12
  1234.1 77.3 reduce-scatter.20
